TPU v7x, 32 devices: a whole 2x2x4 slice. The times are simulated.
32 devices in a mesh: expert: 4 (over y, core), shard: 8 (over z, x).
Axes of the slice: x: 2, y: 2, z: 4, core: 2. Of those that a mesh axis runs over, the one named last changes fastest.
Arguments:
- train_down: float32 [16, 6400, 4096], P('expert', None, 'shard'), may hold values from -0.109375 to 0.109375
- other_down: bfloat16 [16, 6400, 4096], P('expert', None, 'shard'), may hold values from -0.0390625 to 0.0390625
- router_weight: float32 [4096, 16], P('shard', 'expert'), may hold values from -0.09375 to 0.09375
- router_gain: float32 [4096], P('shard'), may hold values from 0.25 to 1.75
Outputs:
- ready_down: bfloat16 [16, 6400, 4096], P('expert', 'shard')
- scale_down: float32 [16, 6400], P('expert', 'shard')
- serve_router: bfloat16 [4096, 16], replicated
All inputs are finite; a program needn't handle non-finite values.
Results may differ from a plain program's by a relative error of at most 0.001.
Values may be sent and summed in bfloat16 or wider, within the bound.
A program may use at most 256 MiB of HBM per device.

v0:
```python
import jax
import jax.numpy as jnp
from jax import lax
from jax.sharding import PartitionSpec as P


def per_device(train_down, other_down, router_weight, router_gain):
    latest_down = train_down + other_down.astype(jnp.float32)
    total_down = lax.psum(jnp.sum(latest_down * latest_down, axis=2), "shard")
    scale_down = jnp.sqrt(total_down)
    narrow_down = (latest_down / jnp.expand_dims(scale_down, 2)).astype(jnp.bfloat16)
    ready_down = lax.all_to_all(narrow_down, "shard", split_axis=1, concat_axis=2, tiled=True)
    scale_down = lax.dynamic_slice_in_dim(
        scale_down, lax.axis_index("shard") * ready_down.shape[1], ready_down.shape[1], axis=1
    )
    part_router = (router_weight * router_gain[:, None]).astype(jnp.bfloat16)
    row_router = lax.all_gather(part_router, "shard", axis=0, tiled=True)
    serve_router = lax.all_gather(row_router, "expert", axis=1, tiled=True)
    return (ready_down, scale_down, serve_router)


def solution(mesh):
    in_specs = (
        P("expert", None, "shard"),
        P("expert", None, "shard"),
        P("shard", "expert"),
        P("shard"),
    )
    out_specs = (P("expert", "shard", None), P("expert", "shard"), P())
    return jax.shard_map(
        per_device, mesh=mesh, in_specs=in_specs, out_specs=out_specs, check_vma=False
    )
```

profile of v0, /device:TPU:0, one launch (start us, length us, event | category | flops | bytes accessed | tf_op | source)
XLA Modules:
  0.0 905.5 jit_solution(8188198296431997854)
XLA Ops:
  7.2 0.0 all-reduce.2.cloned.1.call-start
  7.2 24.2 %multiply_reduce_fusion = f32[4,6400]{1,0:T(4,128)S(1)} fusion(f32[4,6400,512]{2,1,0:T(8,128)} %param.4, bf16[4,6400,512]{2,1,0:T(8,128)(2,1)} %param.5), kind=kLoop, calls=%fused_computation.1 | loop fusion | flops 52403200 | bytes 78745600 | tf_op jit(solution)/shard_map/reduce_sum | solution.py:9
  31.4 2.3 copy.21
  33.7 0.0 all-reduce.2.cloned.1.call-update
  33.7 135.6 %all-reduce.2.cloned.1.call-done = f32[4,6400]{0,1:T(8,128)} async-done(((f32[4,6400]{0,1:T(8,128)}), f32[4,6400]{0,1:T(8,128)}) %all-reduce.2.cloned.1.call-update) | async-done | bytes 102416 | tf_op jit(solution)/shard_map/psum | solution.py:9
  169.3 2.7 sqrt.3
  172.0 1.2 copy.17
  173.3 34.3 %divide_convert_fusion = bf16[4,6400,512]{2,1,0:T(8,128)(2,1)} fusion(f32[4,6400,512]{2,1,0:T(8,128)} %param.4, bf16[4,6400,512]{2,1,0:T(8,128)(2,1)} %param.5, f32[4,6400]{1,0:T(4,128)S(1)} %copy.17), kind=kLoop, calls=%fused_computation | loop fusion | flops 52428800 | bytes 104960000 | tf_op jit(solution)/shard_map/convert_element_type | solution.py:11
  207.5 33.4 %copy.18 = bf16[4,6400,512]{2,0,1:T(4,128)(2,1)} copy(bf16[4,6400,512]{2,1,0:T(8,128)(2,1)} %divide_convert_fusion) | data formatting | bytes 52428800 | tf_op jit(solution)/shard_map/convert_element_type | solution.py:11
  240.9 0.0 copy-start
  240.9 0.0 copy-start.1
  240.9 6.6 all-to-all-start
  247.6 0.0 copy-done
  247.6 0.0 copy-done.1
  247.6 585.0 %all_gather.6 = bf16[4096,4]{0,1:T(4,128)(2,1)S(1)} all-gather(bf16[512,4]{0,1:T(4,128)(2,1)S(1)} %multiply_convert_fusion), channel_id=1, replica_groups=mesh['expert'=4,'shard'=8] {'shard'}, dimensions={0}, use_global_device_ids=true | all-gather | bytes 36864 | tf_op jit(solution)/shard_map/all_gather | solution.py:17
  832.7 5.4 all-gather
  838.1 0.7 reshape.9
  838.8 0.8 constant_dynamic-slice_fusion
  839.5 1.8 copy.20
  841.3 0.0 all-to-all-done
  841.3 18.2 %copy.19 = bf16[4,800,8,512]{3,2,1,0:T(8,128)(2,1)} copy(bf16[4,800,8,512]{3,0,1,2:T(4,128)(2,1)} %bitcast.1) | data formatting | bytes 52428800 | tf_op jit(solution)/shard_map/all_to_all | solution.py:12
  859.5 39.2 %all_to_all.16 = bf16[4,800,4096]{2,1,0:T(8,128)(2,1)} reshape(bf16[4,800,8,512]{3,2,1,0:T(8,128)(2,1)} %copy.19) | data formatting | bytes 52428800 | tf_op jit(solution)/shard_map/all_to_all | solution.py:12
  (1 shorter events, 0.0 us)
Async XLA Ops:
  7.2 162.2 %all-reduce.2.cloned.1.call-start = ((), (), s32[]{:S(2)}) async-start(), calls=%async_computation.1 | async-start | bytes 6553600 | tf_op jit(solution)/shard_map/psum | solution.py:9
  240.9 6.7 copy-start
  240.9 6.7 copy-start.1
  240.9 600.4 %all-to-all-start = ((bf16[4,6400,512]{2,0,1:T(4,128)(2,1)}), bf16[4,6400,512]{2,0,1:T(4,128)(2,1)}, u32[]{:S(2)}, u32[]{:S(2)}) async-start(bf16[4,6400,512]{2,0,1:T(4,128)(2,1)} %copy.18), calls=%async_computation | async-start | bytes 52428800 | tf_op jit(solution)/shard_map/all_to_all | solution.py:12
Sparse Core Ops, SparseCore 0:
  33.9 135.4 all-reduce.1
where the time goes:
time: 907 us; the launch traced here: 906 us
  blocking collectives  590 us (65%)
  waiting for transfers between devices  136 us (15%)
  local copies, waits for them, and re-layouts  100 us (11%)
  other arithmetic  58.5 us (6%)
  between operations  14.1 us (2%)
    all_gather x1, blocking collectives, per_device(): row_router = lax.all_gather(part_router, 'shard', axis=0, tiled=True)  585 us
    psum x1, waiting for transfers between devices, per_device(): total_down = lax.psum(jnp.sum(latest_down * latest_down, axis=2), 'shard')  136 us
    all_to_all x2, local copies, waits for them, and re-layouts, per_device(): lax.all_to_all(narrow_down, 'shard', split_axis=1, concat_axis=2, tiled=T...  57.4 us
    convert_element_type x1, other arithmetic, per_device(): (latest_down / jnp.expand_dims(scale_down, 2)).astype(jnp.bfloat16)  34.3 us
    convert_element_type x1, local copies, waits for them, and re-layouts, per_device(): (latest_down / jnp.expand_dims(scale_down, 2)).astype(jnp.bfloat16)  33.4 us
    reduce_sum x1, other arithmetic, per_device(): total_down = lax.psum(jnp.sum(latest_down * latest_down, axis=2), 'shard')  24.2 us
  transfers between devices with their start and end apart: 2, of which 1 were waited for; matrix products, arithmetic and copies ran while one was open for 0% of the time, Pallas kernels for 0%

commit v1 on v0

--- a/solution.py
+++ b/solution.py
@@ -14,7 +14,14 @@
         scale_down, lax.axis_index("shard") * ready_down.shape[1], ready_down.shape[1], axis=1
     )
     part_router = (router_weight * router_gain[:, None]).astype(jnp.bfloat16)
-    row_router = lax.all_gather(part_router, "shard", axis=0, tiled=True)
+    ring = [part_router]
+    for hop in range(7):
+        ring.append(lax.ppermute(ring[-1], "shard", [(dev, (dev + 1) % 8) for dev in range(8)]))
+    row_router = jnp.roll(
+        jnp.concatenate(ring[::-1], axis=0),
+        (lax.axis_index("shard") + 1) * ring[0].shape[0],
+        axis=0,
+    )
     serve_router = lax.all_gather(row_router, "expert", axis=1, tiled=True)
     return (ready_down, scale_down, serve_router)
 

time: 907 us -> 912 us (level)
  blocking collectives: 590 us -> 5.42 us
  waiting for transfers between devices: 136 us -> 589 us
  starting transfers between devices: 6.67 us -> 143 us
    all_gather x1 -> x0, blocking collectives: 585 us -> none  [per_device(): row_router = lax.all_gather(part_router, 'shard', axis=0, tiled=True)]
    ppermute x0 -> x7, waiting for transfers between devices: none -> 453 us  [per_device(): lax.ppermute(ring[-1], 'shard', [(dev, (dev + 1) % 8) for dev in range(8)])]
    ppermute x0 -> x7, starting transfers between devices: none -> 136 us  [per_device(): lax.ppermute(ring[-1], 'shard', [(dev, (dev + 1) % 8) for dev in range(8)])]
  transfers between devices with their start and end apart: 2 -> 9, of which waited for: 1 -> 8; matrix products, arithmetic and copies ran while one was open for 0% -> 0% of each run, Pallas kernels for 0% -> 0%
where the time goes in v1:
time: 912 us; the launch traced here: 911 us
  waiting for transfers between devices  589 us (65%)
  starting transfers between devices  143 us (16%)
  local copies, waits for them, and re-layouts  100 us (11%)
  other arithmetic  58.6 us (6%)
  between operations  14.1 us (2%)
    ppermute x7, waiting for transfers between devices, per_device(): lax.ppermute(ring[-1], 'shard', [(dev, (dev + 1) % 8) for dev in range(8)])  453 us
    ppermute x7, starting transfers between devices, per_device(): lax.ppermute(ring[-1], 'shard', [(dev, (dev + 1) % 8) for dev in range(8)])  136 us
    psum x1, waiting for transfers between devices, per_device(): total_down = lax.psum(jnp.sum(latest_down * latest_down, axis=2), 'shard')  136 us
    all_to_all x2, local copies, waits for them, and re-layouts, per_device(): lax.all_to_all(narrow_down, 'shard', split_axis=1, concat_axis=2, tiled=T...  57.4 us
    convert_element_type x1, other arithmetic, per_device(): (latest_down / jnp.expand_dims(scale_down, 2)).astype(jnp.bfloat16)  34.3 us
    convert_element_type x1, local copies, waits for them, and re-layouts, per_device(): (latest_down / jnp.expand_dims(scale_down, 2)).astype(jnp.bfloat16)  33.4 us
    reduce_sum x1, other arithmetic, per_device(): total_down = lax.psum(jnp.sum(latest_down * latest_down, axis=2), 'shard')  24.2 us
  transfers between devices with their start and end apart: 9, of which 8 were waited for; matrix products, arithmetic and copies ran while one was open for 0% of the time, Pallas kernels for 0%

profile of v1, /device:TPU:0, one launch (start us, length us, event | category | flops | bytes accessed | tf_op | source)
XLA Modules:
  0.0 910.6 jit_solution(641777327803930614)
XLA Ops:
  7.2 0.0 all-reduce.2.cloned.1.call-start
  7.2 24.2 %multiply_reduce_fusion = f32[4,6400]{1,0:T(4,128)S(1)} fusion(f32[4,6400,512]{2,1,0:T(8,128)} %param.4, bf16[4,6400,512]{2,1,0:T(8,128)(2,1)} %param.5), kind=kLoop, calls=%fused_computation.1 | loop fusion | flops 52403200 | bytes 78745600 | tf_op jit(solution)/shard_map/reduce_sum | solution.py:9
  31.4 2.3 copy.21
  33.7 0.0 all-reduce.2.cloned.1.call-update
  33.7 135.6 %all-reduce.2.cloned.1.call-done = f32[4,6400]{0,1:T(8,128)} async-done(((f32[4,6400]{0,1:T(8,128)}), f32[4,6400]{0,1:T(8,128)}) %all-reduce.2.cloned.1.call-update) | async-done | bytes 102416 | tf_op jit(solution)/shard_map/psum | solution.py:9
  169.3 2.7 sqrt.3
  172.0 1.2 copy.17
  173.3 34.3 %divide_convert_fusion = bf16[4,6400,512]{2,1,0:T(8,128)(2,1)} fusion(f32[4,6400,512]{2,1,0:T(8,128)} %param.4, bf16[4,6400,512]{2,1,0:T(8,128)(2,1)} %param.5, f32[4,6400]{1,0:T(4,128)S(1)} %copy.17), kind=kLoop, calls=%fused_computation | loop fusion | flops 52428800 | bytes 104960000 | tf_op jit(solution)/shard_map/convert_element_type | solution.py:11
  207.5 33.4 %copy.18 = bf16[4,6400,512]{2,0,1:T(4,128)(2,1)} copy(bf16[4,6400,512]{2,1,0:T(8,128)(2,1)} %divide_convert_fusion) | data formatting | bytes 52428800 | tf_op jit(solution)/shard_map/convert_element_type | solution.py:11
  241.0 0.0 copy-start
  241.0 0.0 copy-start.1
  241.0 6.7 all-to-all-start
  247.6 0.0 copy-done
  247.6 0.0 copy-done.1
  247.7 1.9 collective-permute-start
  249.6 424.6 %collective-permute-done = bf16[512,4]{0,1:T(4,128)(2,1)S(1)} collective-permute-done((bf16[512,4]{0,1:T(4,128)(2,1)S(1)}, bf16[512,4]{0,1:T(4,128)(2,1)S(1)}, u32[]{:S(2)}, u32[]{:S(2)}) %collective-permute-start) | collective-permute-done | bytes 4128 | tf_op jit(solution)/shard_map/ppermute | solution.py:19
  674.2 0.0 collective-permute-start.1
  674.2 6.4 collective-permute-done.1
  680.6 0.0 collective-permute-start.2
  680.6 6.4 collective-permute-done.2
  687.0 129.9 %collective-permute-start.3 = (bf16[512,4]{0,1:T(4,128)(2,1)S(1)}, bf16[512,4]{0,1:T(4,128)(2,1)S(1)}, u32[]{:S(2)}, u32[]{:S(2)}) collective-permute-start(bf16[512,4]{0,1:T(4,128)(2,1)S(1)} %collective-permute-done.2), channel_id=1, source_target_pairs={{0,1},{1,2},{2,3},{3,4},{4,5},{5,6},{6,7},{7,0},{8,9},{9,10},{10,1... | collective-permute-start | bytes 12296 | tf_op jit(solution)/shard_map/ppermute | solution.py:19
  817.0 1.3 collective-permute-done.3
  818.3 3.3 collective-permute-start.4
  821.6 3.2 collective-permute-done.4
  824.9 1.3 collective-permute-start.5
  826.1 5.0 collective-permute-done.5
  831.2 0.0 collective-permute-start.6
  831.2 6.3 collective-permute-done.6
  837.7 5.4 all-gather
  843.1 0.7 reshape.9
  843.8 0.8 constant_dynamic-slice_fusion
  844.6 1.8 copy.20
  846.4 0.0 all-to-all-done
  846.4 18.2 %copy.19 = bf16[4,800,8,512]{3,2,1,0:T(8,128)(2,1)} copy(bf16[4,800,8,512]{3,0,1,2:T(4,128)(2,1)} %bitcast.1) | data formatting | bytes 52428800 | tf_op jit(solution)/shard_map/all_to_all | solution.py:12
  864.6 39.2 %all_to_all.16 = bf16[4,800,4096]{2,1,0:T(8,128)(2,1)} reshape(bf16[4,800,8,512]{3,2,1,0:T(8,128)(2,1)} %copy.19) | data formatting | bytes 52428800 | tf_op jit(solution)/shard_map/all_to_all | solution.py:12
  (18 shorter events, 0.2 us)
Async XLA Ops:
  7.2 162.2 %all-reduce.2.cloned.1.call-start = ((), (), s32[]{:S(2)}) async-start(), calls=%async_computation.1 | async-start | bytes 6553600 | tf_op jit(solution)/shard_map/psum | solution.py:9
  241.0 6.7 copy-start
  241.0 6.7 copy-start.1
  241.0 605.4 %all-to-all-start = ((bf16[4,6400,512]{2,0,1:T(4,128)(2,1)}), bf16[4,6400,512]{2,0,1:T(4,128)(2,1)}, u32[]{:S(2)}, u32[]{:S(2)}) async-start(bf16[4,6400,512]{2,0,1:T(4,128)(2,1)} %copy.18), calls=%async_computation | async-start | bytes 52428800 | tf_op jit(solution)/shard_map/all_to_all | solution.py:12
  247.7 426.6 %collective-permute-start = (bf16[512,4]{0,1:T(4,128)(2,1)S(1)}, bf16[512,4]{0,1:T(4,128)(2,1)S(1)}, u32[]{:S(2)}, u32[]{:S(2)}) collective-permute-start(bf16[512,4]{0,1:T(4,128)(2,1)S(1)} %multiply_convert_fusion), channel_id=1, source_target_pairs={{0,1},{1,2},{2,3},{3,4},{4,5},{5,6},{6,7},{7,0},{8,9},{9,10},{10,1... | collective-permute-start | bytes 12296 | tf_op jit(solution)/shard_map/ppermute | solution.py:19
  674.2 6.4 collective-permute-start.1
  680.6 6.4 collective-permute-start.2
  687.0 131.3 %collective-permute-start.3 = (bf16[512,4]{0,1:T(4,128)(2,1)S(1)}, bf16[512,4]{0,1:T(4,128)(2,1)S(1)}, u32[]{:S(2)}, u32[]{:S(2)}) collective-permute-start(bf16[512,4]{0,1:T(4,128)(2,1)S(1)} %collective-permute-done.2), channel_id=1, source_target_pairs={{0,1},{1,2},{2,3},{3,4},{4,5},{5,6},{6,7},{7,0},{8,9},{9,10},{10,1... | collective-permute-start | bytes 12296 | tf_op jit(solution)/shard_map/ppermute | solution.py:19
  818.3 6.6 collective-permute-start.4
  824.9 6.3 collective-permute-start.5
  831.2 6.3 collective-permute-start.6
Sparse Core Ops, SparseCore 0:
  33.9 135.4 all-reduce.1
